TPU v7x, 512 devices: a 8x2x16 block of a 8x8x16 slice. The times are simulated.
512 devices in a mesh: groups: 2 (over y), seq: 16 (over z), tensor: 8 (over x), sub: 2 (over core).
Axes of the slice: x: 8, y: 2, z: 16, core: 2. Of those that a mesh axis runs over, the one named last changes fastest.
The devices are a block of a 8x8x16 slice.
Arguments:
- image_tokens: bfloat16 [8192, 3072], P(('groups', 'seq')), parts along dimension 0, may hold values from -6 to 6
- text_tokens: bfloat16 [1024, 3072], P(('groups', 'seq')), parts along dimension 0, may hold values from -6 to 6
- timestep: int32 [2], P('groups'), parts along dimension 0, may hold values from 0 to 49
- text_length: int32 [2], P('groups'), parts along dimension 0, may hold values from 128 to 512
- time_table: bfloat16 [50, 3072], replicated, may hold values from -6 to 6
- mod_weight: bfloat16 [3072, 18432], P('seq', ('tensor', 'sub')), may hold values from -0.109375 to 0.109375
- qkv_image: bfloat16 [3072, 6144], P('seq', ('tensor', 'sub')), as said below
- qkv_text: bfloat16 [3072, 6144], P('seq', ('tensor', 'sub')), as said below
- norm_gain: float32 [2, 2, 16, 128], P(None, None, ('tensor', 'sub')), may hold values from 1 to 6
- proj_image: bfloat16 [2048, 3072], P(('tensor', 'sub'), 'seq'), may hold values from -0.125 to 0.125
- proj_text: bfloat16 [2048, 3072], P(('tensor', 'sub'), 'seq'), may hold values from -0.125 to 0.125
Outputs:
- image_out: bfloat16 [8192, 3072], P(('groups', 'seq'), ('tensor', 'sub')), parts along dimension 0
- text_out: bfloat16 [1024, 3072], P(('groups', 'seq'), ('tensor', 'sub')), parts along dimension 0
There are 2 independent parts, one for each index of `groups`. A program takes and returns all parts, laid end to end along the dimension named above; an argument that names none is the same for every part. Nothing has to cross between parts.
Inputs may be any that keep to these rules, and one draw needn't show every extreme that they name: `qkv_image`: entries of standard deviation about 1/sqrt(3072). `qkv_text`: entries of standard deviation about 1/sqrt(3072).
All inputs are finite; a program needn't handle non-finite values.
Results may differ from a plain program's by a relative error of at most 0.0085.
Values may be sent and summed in bfloat16 or wider, within the bound.
A program may use at most 64 MiB of HBM per device.

v0:
```python
import jax
import jax.numpy as jnp
from jax import lax
from jax.sharding import PartitionSpec as P

EPSILON = 1e-06


def copy_for_each(x, axis):
    copies = jnp.broadcast_to(x, (lax.axis_size(axis), *x.shape))
    return lax.all_to_all(copies, axis, split_axis=0, concat_axis=0, tiled=True)


def over_copies(x, axis):
    everything = copy_for_each(x, axis)
    return jnp.sum(everything, axis=0)


def side_by_side(arrays, axis, dim, along):
    ends, at = ([], 0)
    for a in arrays[:-1]:
        at += a.shape[along]
        ends.append(at)
    both = jnp.concatenate(arrays, axis=along)
    return tuple(jnp.split(lax.all_gather(both, axis, axis=dim, tiled=True), ends, axis=along))


def joined_along(tiles, dim):
    shape = list(tiles.shape[1:])
    shape[dim] *= tiles.shape[0]
    return jnp.moveaxis(tiles, 0, dim).reshape(shape)


def gather_directly(x, axis, dim):
    return joined_along(copy_for_each(x, axis), dim)


def modulate(tokens, shift, scaling):
    values = tokens.astype(jnp.float32)
    center = jnp.mean(values, axis=-1, keepdims=True)
    spread = jnp.mean(jnp.square(values - center), axis=-1, keepdims=True)
    normed = (values - center) * lax.rsqrt(spread + EPSILON)
    return (normed * (1.0 + scaling) + shift).astype(jnp.bfloat16)


def head_norm(values, gain):
    return values * lax.rsqrt(jnp.mean(values * values, axis=-1, keepdims=True) + EPSILON) * gain


def split_heads(projected, gains):
    shaped = projected.reshape(projected.shape[0], -1, 3, gains.shape[-1])
    queries = head_norm(shaped[:, :, 0], gains[0]).astype(jnp.bfloat16)
    keys = head_norm(shaped[:, :, 1], gains[1]).astype(jnp.bfloat16)
    values = shaped[:, :, 2].astype(jnp.bfloat16)
    return (queries, keys, values)


def add_rows(source, shards):
    return jnp.dot(source, shards, preferred_element_type=jnp.float32)


def body(
    image_tokens,
    text_tokens,
    timestep,
    text_length,
    time_table,
    mod_weight,
    qkv_image,
    qkv_text,
    norm_gain,
    proj_image,
    proj_text,
):
    columns_all = image_tokens.shape[1]
    embedded = lax.dynamic_index_in_dim(time_table, timestep[0], 0, keepdims=False).astype(
        jnp.float32
    )
    vector = jax.nn.silu(embedded).astype(jnp.bfloat16)
    slab_rows = mod_weight.shape[0]
    vector_rows = lax.dynamic_slice_in_dim(vector, lax.axis_index("seq") * slab_rows, slab_rows)
    partial_value = jnp.dot(vector_rows[None, :], mod_weight, preferred_element_type=jnp.float32)[0]
    summed_rows = over_copies(partial_value, "seq")
    modulation = lax.all_gather(summed_rows, ("tensor", "sub"), axis=0, tiled=True)
    modulation = modulation.reshape(2, 3, columns_all)
    hidden_image = modulate(image_tokens, modulation[0, 0], modulation[0, 1])
    hidden_text = modulate(text_tokens, modulation[1, 0], modulation[1, 1])
    image_count = image_tokens.shape[0]
    text_count = text_tokens.shape[0]
    local_rows = image_count + text_count
    shards = side_by_side((qkv_image, qkv_text), "seq", 0, 1)
    projected_image = add_rows(hidden_image, shards[0])
    projected_text = add_rows(hidden_text, shards[1])
    image_q, image_k, image_v = split_heads(projected_image, norm_gain[0])
    text_q, text_k, text_v = split_heads(projected_text, norm_gain[1])
    heads_here = image_q.shape[1]
    head_size = image_q.shape[2]
    queries = jnp.concatenate([text_q, image_q], axis=0)
    keys = jnp.concatenate([text_k, image_k], axis=0)
    values = jnp.concatenate([text_v, image_v], axis=0)
    keys_values = jnp.stack([keys, values], axis=2).reshape(local_rows, heads_here * 2 * head_size)
    factor = float(head_size) ** (-0.5)
    shards = lax.all_gather(keys_values, "seq", axis=0, tiled=True)
    count = shards.shape[0]
    blocks = shards.reshape(count, heads_here, 2, head_size)
    position = jnp.arange(count, dtype=jnp.int32)
    within = position % local_rows
    owner = position // local_rows
    usable = (within >= text_count) | (owner * text_count + within < text_length[0])
    scores = (
        jnp.einsum("qhd,khd->hqk", queries, blocks[:, :, 0], preferred_element_type=jnp.float32)
        * factor
    )
    scores = jnp.where(usable[None, None, :], scores, -1e30)
    run_max = jnp.full((heads_here, local_rows), -1e30, jnp.float32)
    new_max = jnp.maximum(run_max, jnp.max(scores, axis=-1))
    probs = jnp.exp(scores - new_max[:, :, None])
    run_sum = jnp.sum(probs, axis=-1)
    totals = jnp.einsum(
        "hqk,khd->hqd",
        probs.astype(jnp.bfloat16),
        blocks[:, :, 1],
        preferred_element_type=jnp.float32,
    )
    final_max, run_sum, totals = (new_max, run_sum, totals)
    attended = (
        (totals / run_sum[:, :, None])
        .astype(jnp.bfloat16)
        .transpose(1, 0, 2)
        .reshape(local_rows, heads_here * head_size)
    )
    stacked = jnp.stack([proj_image, proj_text], axis=0)
    width_here = columns_all // lax.axis_size(("tensor", "sub"))
    first = lax.axis_index(("tensor", "sub")) * width_here
    attended_all = lax.all_gather(attended, ("tensor", "sub"), axis=1, tiled=True)
    full_columns = gather_directly(stacked, "seq", 2)
    all_rows = lax.all_to_all(
        full_columns, ("tensor", "sub"), split_axis=2, concat_axis=1, tiled=True
    )
    text_part = jnp.dot(attended_all[:text_count], all_rows[1], preferred_element_type=jnp.float32)
    image_part = jnp.dot(attended_all[text_count:], all_rows[0], preferred_element_type=jnp.float32)
    summed = jnp.concatenate([text_part, image_part], axis=0)
    gates = lax.dynamic_slice_in_dim(modulation[:, 2], first, width_here, 1)
    image_base = lax.dynamic_slice_in_dim(image_tokens, first, width_here, 1).astype(jnp.float32)
    text_base = lax.dynamic_slice_in_dim(text_tokens, first, width_here, 1).astype(jnp.float32)
    image_out = (image_base + gates[0] * summed[text_count:]).astype(jnp.bfloat16)
    text_out = (text_base + gates[1] * summed[:text_count]).astype(jnp.bfloat16)
    return (image_out, text_out)


def solution(mesh):
    return jax.shard_map(
        body,
        mesh=mesh,
        in_specs=(
            P(("groups", "seq"), None),
            P(("groups", "seq"), None),
            P("groups"),
            P("groups"),
            P(),
            P("seq", ("tensor", "sub")),
            P("seq", ("tensor", "sub")),
            P("seq", ("tensor", "sub")),
            P(None, None, ("tensor", "sub"), None),
            P(("tensor", "sub"), "seq"),
            P(("tensor", "sub"), "seq"),
        ),
        out_specs=(
            P(("groups", "seq"), ("tensor", "sub")),
            P(("groups", "seq"), ("tensor", "sub")),
        ),
        check_vma=False,
    )
```

profile of v0, /device:TPU:65, one launch (start us, length us, event | category | flops | bytes accessed | tf_op | source)
XLA Modules:
  0.0 331.8 jit_solution(2012975773529519492)
XLA Ops:
  7.3 1.8 pad_maximum_fusion
  11.6 44.2 %all-to-all-start = ((f32[16,1,1152]{2,1,0:T(1,128)}), f32[16,1,1152]{2,1,0:T(1,128)S(1)}, u32[]{:S(2)}, u32[]{:S(2)}) async-start(f32[16,1,1152]{2,1,0:T(1,128)} %broadcast_in_dim.14), calls=%async_computation | async-start | bytes 147456 | tf_op jit(solution)/shard_map/all_to_all | solution.py:11
  55.9 1.1 convert_reduce_fusion.1
  56.9 1.2 fusion.38
  59.1 8.3 %all-to-all-done = f32[16,1,1152]{2,1,0:T(1,128)S(1)} async-done(((f32[16,1,1152]{2,1,0:T(1,128)}), f32[16,1,1152]{2,1,0:T(1,128)S(1)}, u32[]{:S(2)}, u32[]{:S(2)}) %all-to-all-start) | async-done | bytes 73760 | tf_op jit(solution)/shard_map/all_to_all | solution.py:11
  67.4 1.5 broadcast_in_dim.22
  68.9 4.8 %all-to-all-start.1 = ((bf16[16,2,128,192]{2,3,1,0:T(8,128)(2,1)}), bf16[16,2,128,192]{2,3,1,0:T(8,128)(2,1)}, u32[]{:S(2)}, u32[]{:S(2)}) async-start(bf16[16,2,128,192]{2,3,1,0:T(8,128)(2,1)} %broadcast_in_dim.22), calls=%async_computation.1 | async-start | bytes 3145728 | tf_op jit(solution)/shard_map/all_to_all | solution.py:11
  73.8 20.3 %all-gather = f32[16,1,1152]{2,1,0:T(1,128)S(1)} all-gather(f32[1,1,1152]{2,1,0:T(1,128)S(1)} %reshape.562), channel_id=1, replica_groups=mesh['groups'=2,'seq'=16,'tensor'=8,'sub'=2] {'tensor','sub'}, dimensions={0}, use_global_device_ids=true | all-gather | bytes 78336 | tf_op jit(solution)/shard_map/all_gather | solution.py:84
  94.4 90.3 %all-gather.5.cloned.1.call-done = bf16[3072,768]{1,0:T(8,128)(2,1)} async-done(((bf16[192,768]{1,0:T(8,128)(2,1)}), bf16[3072,768]{1,0:T(8,128)(2,1)}) %all-gather.5.cloned.1.call-update) | async-done | bytes 4718608 | tf_op jit(solution)/shard_map/all_gather | solution.py:25
  184.7 2.2 fusion.14
  187.4 3.0 fusion.12
  192.3 1.5 copy.69
  193.9 13.8 %copy.70 = bf16[2,128,3072]{1,0,2:T(2,128)(2,1)} copy(bf16[2,128,3072]{1,2,0:T(8,128)(2,1)S(1)} %bitcast.86) | data formatting | bytes 3145728 | tf_op jit(solution)/shard_map/reshape | solution.py:31
  207.7 13.5 %all-to-all-start.2 = ((bf16[2,128,3072]{1,0,2:T(2,128)(2,1)}), bf16[2,128,3072]{1,0,2:T(2,128)(2,1)}, u32[]{:S(2)}, u32[]{:S(2)}) async-start(bf16[2,128,3072]{1,0,2:T(2,128)(2,1)} %copy.70), calls=%async_computation.2 | async-start | bytes 3145728 | tf_op jit(solution)/shard_map/all_to_all | solution.py:137
  221.7 38.3 %all-gather.7.cloned.1.call-done = bf16[4608,256]{1,0:T(8,128)(2,1)} async-done(((bf16[288,256]{1,0:T(8,128)(2,1)}), bf16[4608,256]{1,0:T(8,128)(2,1)}) %all-gather.7.cloned.1.call-update) | async-done | bytes 2359312 | tf_op jit(solution)/shard_map/all_gather | solution.py:103
  260.0 4.6 %reshape.557 = bf16[4608,1,2,128]{3,2,0,1:T(2,128)(2,1)S(1)} reshape(bf16[4608,256]{1,0:T(8,128)(2,1)} %all-gather.7.cloned.1.call-done) | data formatting | bytes 4718592 | tf_op jit(solution)/shard_map/reshape | solution.py:105
  264.7 3.4 %fusion.63 = (bf16[4608,1,1,128]{3,2,0,1:T(2,128)(2,1)S(1)}, bf16[4608,1,1,128]{3,2,0,1:T(2,128)(2,1)S(1)}) fusion(bf16[4608,1,2,128]{3,2,0,1:T(2,128)(2,1)S(1)} %reshape.557), kind=kLoop, calls=%fused_computation.110 | loop fusion | bytes 4718592 | tf_op jit(solution)/shard_map/slice | solution.py:111
  268.1 1.3 fusion.66
  270.2 1.6 fusion.28
  271.8 1.0 constant_dynamic-slice_fusion.2
  273.1 1.6 copy.71
  275.9 45.1 %all-gather.9.cloned.1.call-done = bf16[288,2048]{1,0:T(8,128)(2,1)} async-done(((bf16[288,128]{1,0:T(8,128)(2,1)}), bf16[288,2048]{1,0:T(8,128)(2,1)}) %all-gather.9.cloned.1.call-update) | async-done | bytes 1179664 | tf_op jit(solution)/shard_map/all_gather | solution.py:135
  321.0 1.9 fusion.24
  322.9 2.4 fusion.22
  (67 shorter events, 7.8 us)
Async XLA Ops:
  7.2 3.6 %copy-start = (bf16[192,1152]{1,0:T(8,128)(2,1)S(1)}, bf16[192,1152]{1,0:T(8,128)(2,1)}, u32[]{:S(2)}) copy-start(bf16[192,1152]{1,0:T(8,128)(2,1)} %param.16) | copy-start | bytes 1327108
  7.2 50.9 %copy-start.1 = (bf16[256,3072]{1,0:T(8,128)(2,1)S(1)}, bf16[256,3072]{1,0:T(8,128)(2,1)}, u32[]{:S(2)}) copy-start(bf16[256,3072]{1,0:T(8,128)(2,1)} %param.11) | copy-start | bytes 4718596
  7.2 177.5 %all-gather.5.cloned.1.call-start = ((), (), s32[]{:S(2)}) async-start(), calls=%async_computation.3 | async-start | bytes 5013504 | tf_op jit(solution)/shard_map/all_gather | solution.py:25
  9.1 49.9 %copy-start.3 = (bf16[128,192]{0,1:T(8,128)(2,1)S(1)}, bf16[128,192]{0,1:T(8,128)(2,1)}, u32[]{:S(2)}) copy-start(bf16[128,192]{0,1:T(8,128)(2,1)} %param.21) | copy-start | bytes 147460
  9.1 49.9 %copy-start.4 = (bf16[128,192]{0,1:T(8,128)(2,1)S(1)}, bf16[128,192]{0,1:T(8,128)(2,1)}, u32[]{:S(2)}) copy-start(bf16[128,192]{0,1:T(8,128)(2,1)} %param.20) | copy-start | bytes 147460
  9.1 49.9 %copy-start.5 = (f32[2,2,1,128]{3,2,1,0:T(1,128)S(1)}, f32[2,2,1,128]{3,2,1,0:T(1,128)}, u32[]{:S(2)}) copy-start(f32[2,2,1,128]{3,2,1,0:T(1,128)} %param.19) | copy-start | bytes 6148
  11.6 55.7 %all-to-all-start = ((f32[16,1,1152]{2,1,0:T(1,128)}), f32[16,1,1152]{2,1,0:T(1,128)S(1)}, u32[]{:S(2)}, u32[]{:S(2)}) async-start(f32[16,1,1152]{2,1,0:T(1,128)} %broadcast_in_dim.14), calls=%async_computation | async-start | bytes 147456 | tf_op jit(solution)/shard_map/all_to_all | solution.py:11
  59.0 125.6 %copy-start.2 = (bf16[32,3072]{1,0:T(8,128)(2,1)S(1)}, bf16[32,3072]{1,0:T(8,128)(2,1)}, u32[]{:S(2)}) copy-start(bf16[32,3072]{1,0:T(8,128)(2,1)} %param.12) | copy-start | bytes 589828
  68.9 123.5 %all-to-all-start.1 = ((bf16[16,2,128,192]{2,3,1,0:T(8,128)(2,1)}), bf16[16,2,128,192]{2,3,1,0:T(8,128)(2,1)}, u32[]{:S(2)}, u32[]{:S(2)}) async-start(bf16[16,2,128,192]{2,3,1,0:T(8,128)(2,1)} %broadcast_in_dim.22), calls=%async_computation.1 | async-start | bytes 3145728 | tf_op jit(solution)/shard_map/all_to_all | solution.py:11
  73.7 186.4 %all-gather.7.cloned.1.call-start = ((), (), s32[]{:S(2)}) async-start(), calls=%async_computation.4 | async-start | bytes 2506752 | tf_op jit(solution)/shard_map/all_gather | solution.py:103
  207.7 65.4 %all-to-all-start.2 = ((bf16[2,128,3072]{1,0,2:T(2,128)(2,1)}), bf16[2,128,3072]{1,0,2:T(2,128)(2,1)}, u32[]{:S(2)}, u32[]{:S(2)}) async-start(bf16[2,128,3072]{1,0,2:T(2,128)(2,1)} %copy.70), calls=%async_computation.2 | async-start | bytes 3145728 | tf_op jit(solution)/shard_map/all_to_all | solution.py:137
  221.2 99.8 %all-gather.9.cloned.1.call-start = ((), (), s32[]{:S(2)}) async-start(), calls=%async_computation.5 | async-start | bytes 1253376 | tf_op jit(solution)/shard_map/all_gather | solution.py:135
Sparse Core Ops, SparseCore 0:
  10.1 174.5 all-gather.4
  191.8 68.2 all-gather.6
  271.9 49.0 all-gather.8
where the time goes:
time: 333 us; the launch traced here: 332 us
  waiting for transfers between devices  182 us (55%)
  starting transfers between devices  62.9 us (19%)
  local copies, waits for them, and re-layouts  30.8 us (9%)
  blocking collectives  20.3 us (6%)
  between operations  15.4 us (5%)
  matrix products  12.4 us (4%)
  other arithmetic  7.8 us (2%)
    all_gather x1, waiting for transfers between devices, side_by_side(): lax.all_gather(both, axis, axis=dim, tiled=True)  90.3 us
    all_to_all x2, starting transfers between devices, copy_for_each(): return lax.all_to_all(copies, axis, split_axis=0, concat_axis=0, tiled=True)  49 us
    all_gather x1, waiting for transfers between devices, body(): lax.all_gather(attended, ('tensor', 'sub'), axis=1, tiled=True)  45.1 us
    all_gather x1, waiting for transfers between devices, body(): shards = lax.all_gather(keys_values, 'seq', axis=0, tiled=True)  38.3 us
    all_gather x1, blocking collectives, body(): lax.all_gather(summed_rows, ('tensor', 'sub'), axis=0, tiled=True)  20.3 us
    reshape x1, local copies, waits for them, and re-layouts, joined_along(): return jnp.moveaxis(tiles, 0, dim).reshape(shape)  13.8 us
    all_to_all x1, starting transfers between devices, body(): lax.all_to_all(full_columns, ('tensor', 'sub'), split_axis=2, concat_axis...  13.5 us
    all_to_all x2, waiting for transfers between devices, copy_for_each(): return lax.all_to_all(copies, axis, split_axis=0, concat_axis=0, tiled=True)  8.32 us
  transfers between devices with their start and end apart: 6, of which 4 were waited for; matrix products, arithmetic and copies ran while one was open for 14% of the time, Pallas kernels for 0%

commit v1 on v0

--- a/solution.py
+++ b/solution.py
@@ -100,7 +100,9 @@
     values = jnp.concatenate([text_v, image_v], axis=0)
     keys_values = jnp.stack([keys, values], axis=2).reshape(local_rows, heads_here * 2 * head_size)
     factor = float(head_size) ** (-0.5)
-    shards = lax.all_gather(keys_values, "seq", axis=0, tiled=True)
+    shards = jnp.concatenate(
+        lax.all_to_all(jnp.stack([keys_values] * lax.axis_size("seq")), "seq", 0, 0), axis=0
+    )
     count = shards.shape[0]
     blocks = shards.reshape(count, heads_here, 2, head_size)
     position = jnp.arange(count, dtype=jnp.int32)

time: 333 us -> 382 us (1.15)
  waiting for transfers between devices: 182 us -> 231 us
    all_to_all x0 -> x1, waiting for transfers between devices: none -> 86.6 us  [body(): lax.all_to_all(jnp.stack([keys_values] * lax.axis_size('seq')), 'seq', 0, 0)]
    all_gather x1 -> x0, waiting for transfers between devices: 38.3 us -> none  [body(): shards = lax.all_gather(keys_values, 'seq', axis=0, tiled=True)]
    all_gather x1, waiting for transfers between devices: 45.1 us -> 17.5 us  [body(): lax.all_gather(attended, ('tensor', 'sub'), axis=1, tiled=True)]
    all_to_all x1, waiting for transfers between devices: 0.01 us -> 26.1 us  [body(): lax.all_to_all(full_columns, ('tensor', 'sub'), split_axis=2, concat_axis...]
    all_to_all x0 -> x1, starting transfers between devices: none -> 6.71 us  [body(): lax.all_to_all(jnp.stack([keys_values] * lax.axis_size('seq')), 'seq', 0, 0)]
    another operation x0 -> x3, local copies, waits for them, and re-layouts: none -> 6.4 us  [the longest x1 4.63 us: body(): blocks = shards.reshape(count, heads_here, 2, head_size)]
    all_to_all x1, starting transfers between devices: 13.5 us -> 8.06 us  [body(): lax.all_to_all(full_columns, ('tensor', 'sub'), split_axis=2, concat_axis...]
    reshape x2 -> x0, local copies, waits for them, and re-layouts: 5.4 us -> none  [the longest x1 4.63 us: body(): blocks = shards.reshape(count, heads_here, 2, head_size)]
  transfers between devices with their start and end apart: 6 -> 6, of which waited for: 4 -> 5; matrix products, arithmetic and copies ran while one was open for 14% -> 11% of each run, Pallas kernels for 0% -> 0%
where the time goes in v1:
time: 382 us
  waiting for transfers between devices  231 us (60%)
  starting transfers between devices  64.1 us (17%)
  local copies, waits for them, and re-layouts  31.8 us (8%)
  blocking collectives  20.3 us (5%)
  between operations  15.7 us (4%)
  matrix products  12.4 us (3%)
  other arithmetic  6.69 us (2%)
    all_gather x1, waiting for transfers between devices, side_by_side(): lax.all_gather(both, axis, axis=dim, tiled=True)  89.7 us
    all_to_all x1, waiting for transfers between devices, body(): lax.all_to_all(jnp.stack([keys_values] * lax.axis_size('seq')), 'seq', 0, 0)  86.6 us
    all_to_all x2, starting transfers between devices, copy_for_each(): return lax.all_to_all(copies, axis, split_axis=0, concat_axis=0, tiled=True)  49 us
    all_to_all x1, waiting for transfers between devices, body(): lax.all_to_all(full_columns, ('tensor', 'sub'), split_axis=2, concat_axis...  26.1 us
    all_gather x1, blocking collectives, body(): lax.all_gather(summed_rows, ('tensor', 'sub'), axis=0, tiled=True)  20.3 us
    all_gather x1, waiting for transfers between devices, body(): lax.all_gather(attended, ('tensor', 'sub'), axis=1, tiled=True)  17.5 us
    reshape x1, local copies, waits for them, and re-layouts, joined_along(): return jnp.moveaxis(tiles, 0, dim).reshape(shape)  13.8 us
    all_to_all x2, waiting for transfers between devices, copy_for_each(): return lax.all_to_all(copies, axis, split_axis=0, concat_axis=0, tiled=True)  10.6 us
  transfers between devices with their start and end apart: 6, of which 5 were waited for; matrix products, arithmetic and copies ran while one was open for 11% of the time, Pallas kernels for 0%

profile of v1, /device:TPU:65, one launch (start us, length us, event | category | flops | bytes accessed | tf_op | source)
XLA Modules:
  0.0 381.6 jit_solution(5290732427297364250)
XLA Ops:
  7.3 1.8 pad_maximum_fusion
  11.5 44.2 %all-to-all-start = ((f32[16,1,1152]{2,1,0:T(1,128)}), f32[16,1,1152]{2,1,0:T(1,128)S(1)}, u32[]{:S(2)}, u32[]{:S(2)}) async-start(f32[16,1,1152]{2,1,0:T(1,128)} %broadcast_in_dim.14), calls=%async_computation | async-start | bytes 147456 | tf_op jit(solution)/shard_map/all_to_all | solution.py:11
  56.6 10.6 %all-to-all-done = f32[16,1,1152]{2,1,0:T(1,128)S(1)} async-done(((f32[16,1,1152]{2,1,0:T(1,128)}), f32[16,1,1152]{2,1,0:T(1,128)S(1)}, u32[]{:S(2)}, u32[]{:S(2)}) %all-to-all-start) | async-done | bytes 73760 | tf_op jit(solution)/shard_map/all_to_all | solution.py:11
  67.3 1.5 broadcast_in_dim.22
  68.8 4.8 %all-to-all-start.2 = ((bf16[16,2,128,192]{2,3,1,0:T(8,128)(2,1)}), bf16[16,2,128,192]{2,3,1,0:T(8,128)(2,1)}, u32[]{:S(2)}, u32[]{:S(2)}) async-start(bf16[16,2,128,192]{2,3,1,0:T(8,128)(2,1)} %broadcast_in_dim.22), calls=%async_computation.2 | async-start | bytes 3145728 | tf_op jit(solution)/shard_map/all_to_all | solution.py:11
  74.9 20.3 %all-gather = f32[16,1,1152]{2,1,0:T(1,128)S(1)} all-gather(f32[1,1,1152]{2,1,0:T(1,128)S(1)} %reshape.556), channel_id=1, replica_groups=mesh['groups'=2,'seq'=16,'tensor'=8,'sub'=2] {'tensor','sub'}, dimensions={0}, use_global_device_ids=true | all-gather | bytes 78336 | tf_op jit(solution)/shard_map/all_gather | solution.py:84
  95.5 89.7 %all-gather.4.cloned.1.call-done = bf16[3072,768]{1,0:T(8,128)(2,1)} async-done(((bf16[192,768]{1,0:T(8,128)(2,1)}), bf16[3072,768]{1,0:T(8,128)(2,1)}) %all-gather.4.cloned.1.call-update) | async-done | bytes 4718608 | tf_op jit(solution)/shard_map/all_gather | solution.py:25
  185.2 2.2 fusion.14
  187.9 3.0 fusion.12
  191.5 1.6 stack.24
  193.1 6.7 %all-to-all-start.1 = ((bf16[16,288,256]{2,1,0:T(8,128)(2,1)}), bf16[16,288,256]{2,1,0:T(8,128)(2,1)S(1)}, u32[]{:S(2)}, u32[]{:S(2)}) async-start(bf16[16,288,256]{2,1,0:T(8,128)(2,1)} %stack.24), calls=%async_computation.1 | async-start | bytes 4718592 | tf_op jit(solution)/shard_map/all_to_all | solution.py:104
  200.5 1.5 copy.71
  202.0 13.8 %copy.72 = bf16[2,128,3072]{1,0,2:T(2,128)(2,1)} copy(bf16[2,128,3072]{1,2,0:T(8,128)(2,1)S(1)} %bitcast.86) | data formatting | bytes 3145728 | tf_op jit(solution)/shard_map/reshape | solution.py:31
  216.1 86.6 %all-to-all-done.1 = bf16[16,288,256]{2,1,0:T(8,128)(2,1)S(1)} async-done(((bf16[16,288,256]{2,1,0:T(8,128)(2,1)}), bf16[16,288,256]{2,1,0:T(8,128)(2,1)S(1)}, u32[]{:S(2)}, u32[]{:S(2)}) %all-to-all-start.1) | async-done | bytes 2359328 | tf_op jit(solution)/shard_map/all_to_all | solution.py:104
  302.8 8.1 %all-to-all-start.3 = ((bf16[2,128,3072]{1,0,2:T(2,128)(2,1)}), bf16[2,128,3072]{1,0,2:T(2,128)(2,1)}, u32[]{:S(2)}, u32[]{:S(2)}) async-start(bf16[2,128,3072]{1,0,2:T(2,128)(2,1)} %copy.72), calls=%async_computation.3 | async-start | bytes 3145728 | tf_op jit(solution)/shard_map/all_to_all | solution.py:139
  311.1 4.6 %reshape_reshape.3 = bf16[4608,1,2,128]{3,2,0,1:T(2,128)(2,1)S(1)} reshape(bf16[16,288,256]{2,1,0:T(8,128)(2,1)} %copy-done.1) | data formatting | bytes 4718592 | tf_op jit(solution)/shard_map/reshape;reshape | solution.py:107
  315.7 3.4 fusion.71
  319.1 1.2 fusion.74
  321.2 1.6 fusion.34
  324.1 26.1 %all-to-all-done.3 = bf16[2,128,3072]{1,0,2:T(2,128)(2,1)} async-done(((bf16[2,128,3072]{1,0,2:T(2,128)(2,1)}), bf16[2,128,3072]{1,0,2:T(2,128)(2,1)}, u32[]{:S(2)}, u32[]{:S(2)}) %all-to-all-start.3) | async-done | bytes 1572896 | tf_op jit(solution)/shard_map/all_to_all | solution.py:139
  350.2 1.6 copy.73
  353.0 17.5 %all-gather.6.cloned.1.call-done = bf16[288,2048]{1,0:T(8,128)(2,1)} async-done(((bf16[288,128]{1,0:T(8,128)(2,1)}), bf16[288,2048]{1,0:T(8,128)(2,1)}) %all-gather.6.cloned.1.call-update) | async-done | bytes 1179664 | tf_op jit(solution)/shard_map/all_gather | solution.py:137
  370.5 1.9 fusion.28
  372.4 2.4 fusion.26
  (65 shorter events, 9.3 us)
Async XLA Ops:
  7.2 3.5 copy-start
  7.2 178.0 %all-gather.4.cloned.1.call-start = ((), (), s32[]{:S(2)}) async-start(), calls=%async_computation.4 | async-start | bytes 5013504 | tf_op jit(solution)/shard_map/all_gather | solution.py:25
  11.5 55.7 %all-to-all-start = ((f32[16,1,1152]{2,1,0:T(1,128)}), f32[16,1,1152]{2,1,0:T(1,128)S(1)}, u32[]{:S(2)}, u32[]{:S(2)}) async-start(f32[16,1,1152]{2,1,0:T(1,128)} %broadcast_in_dim.14), calls=%async_computation | async-start | bytes 147456 | tf_op jit(solution)/shard_map/all_to_all | solution.py:11
  56.6 17.0 %copy-start.3 = (bf16[32,3072]{1,0:T(8,128)(2,1)S(1)}, bf16[32,3072]{1,0:T(8,128)(2,1)}, u32[]{:S(2)}) copy-start(bf16[32,3072]{1,0:T(8,128)(2,1)} %param.12) | copy-start | bytes 589828
  56.6 17.4 %copy-start.2 = (bf16[256,3072]{1,0:T(8,128)(2,1)S(1)}, bf16[256,3072]{1,0:T(8,128)(2,1)}, u32[]{:S(2)}) copy-start(bf16[256,3072]{1,0:T(8,128)(2,1)} %param.11) | copy-start | bytes 4718596
  68.8 122.7 %all-to-all-start.2 = ((bf16[16,2,128,192]{2,3,1,0:T(8,128)(2,1)}), bf16[16,2,128,192]{2,3,1,0:T(8,128)(2,1)}, u32[]{:S(2)}, u32[]{:S(2)}) async-start(bf16[16,2,128,192]{2,3,1,0:T(8,128)(2,1)} %broadcast_in_dim.22), calls=%async_computation.2 | async-start | bytes 3145728 | tf_op jit(solution)/shard_map/all_to_all | solution.py:11
  73.6 1.3 copy-start.4
  193.1 109.7 %all-to-all-start.1 = ((bf16[16,288,256]{2,1,0:T(8,128)(2,1)}), bf16[16,288,256]{2,1,0:T(8,128)(2,1)S(1)}, u32[]{:S(2)}, u32[]{:S(2)}) async-start(bf16[16,288,256]{2,1,0:T(8,128)(2,1)} %stack.24), calls=%async_computation.1 | async-start | bytes 4718592 | tf_op jit(solution)/shard_map/all_to_all | solution.py:104
  302.8 8.1 %copy-start.1 = (bf16[16,288,256]{2,1,0:T(8,128)(2,1)}, bf16[16,288,256]{2,1,0:T(8,128)(2,1)S(1)}, u32[]{:S(2)}) copy-start(bf16[16,288,256]{2,1,0:T(8,128)(2,1)S(1)} %all-to-all-done.1) | copy-start | bytes 7077892
  302.8 47.5 %all-to-all-start.3 = ((bf16[2,128,3072]{1,0,2:T(2,128)(2,1)}), bf16[2,128,3072]{1,0,2:T(2,128)(2,1)}, u32[]{:S(2)}, u32[]{:S(2)}) async-start(bf16[2,128,3072]{1,0,2:T(2,128)(2,1)} %copy.72), calls=%async_computation.3 | async-start | bytes 3145728 | tf_op jit(solution)/shard_map/all_to_all | solution.py:139
  310.8 59.7 %all-gather.6.cloned.1.call-start = ((), (), s32[]{:S(2)}) async-start(), calls=%async_computation.5 | async-start | bytes 1253376 | tf_op jit(solution)/shard_map/all_gather | solution.py:137
Sparse Core Ops, SparseCore 0:
  10.1 175.0 all-gather.3
  323.0 47.4 all-gather.5
